TPU v7x, 32 devices: a whole 2x2x4 slice. The times are simulated.
32 devices in a mesh: col: 16 (over z, x, core), row: 2 (over y).
Axes of the slice: x: 2, y: 2, z: 4, core: 2. Of those that a mesh axis runs over, the one named last changes fastest.
Arguments:
- blocks: float32 [16, 2, 24, 128, 128], P('col', 'row'), may hold values from -0.21875 to 0.21875
- row_index: int32 [16, 2, 24], P('col', 'row'), may hold values from 0 to 63
- col_index: int32 [16, 2, 24], P('col', 'row'), may hold values from 0 to 23
- counts: int32 [16, 2], P('col', 'row'), may hold values from 12 to 24, as said below
- rhs: float32 [16384], P(('row', 'col')), may hold values from -6 to 6
- lower: float32 [49152], P(('col', 'row')), may hold values from -0.6 to -0.05
- upper: float32 [49152], P(('col', 'row')), may hold values from 0.05 to 0.6
- primal_start: float32 [49152], P(('col', 'row')), may hold values from -0.05 to 0.05
- dual_start: float32 [16384], P(('row', 'col')), may hold values from -4 to 4
Outputs:
- primal: float32 [49152], P(('col', 'row'))
- dual: float32 [16384], P(('row', 'col'))
- norms: float32 [3, 2], replicated
Inputs may be any that keep to these rules, and one draw needn't show every extreme that they name: `counts`: each list has between 12 and 24 live slots; both ends are reached in every draw.
All inputs are finite; a program needn't handle non-finite values.
Results may differ from a plain program's by a relative error of at most 0.0001.
Values sent between devices are 32-bit elements; how exact they have to be, the bound alone decides.
A program may use at most 64 MiB of HBM per device.

v0:
```python
import jax
import jax.numpy as jnp
from jax import lax
from jax.sharding import PartitionSpec as P

ITERS = 3


def local(blocks, row_index, col_index, counts, rhs, lower, upper, primal_start, dual_start):
    slot_count = blocks.shape[2]
    side = blocks.shape[3]
    tiles = blocks.reshape(slot_count, side, side)
    rows = row_index.reshape(slot_count)
    cols = col_index.reshape(slot_count)
    live = (jnp.arange(slot_count, dtype=jnp.int32) < counts.reshape(())).astype(jnp.float32)
    n_col = lax.axis_size("col")
    n_row = lax.axis_size("row")
    primal_len = primal_start.shape[0]
    dual_len = dual_start.shape[0]
    col_blocks = primal_len * n_row // side
    row_blocks = dual_len * n_col // side
    tau = 0.4
    sigma = 0.4
    records = []

    def record(resid_sq, moved_sq):
        total_resid, total_moved = lax.psum((resid_sq, moved_sq), ("col", "row"))
        records.append(jnp.stack([jnp.sqrt(total_resid), jnp.sqrt(total_moved)]))

    primal_group, lower_group, upper_group = (
        lax.all_gather(primal_start, "row", axis=0, tiled=True),
        lax.all_gather(lower, "row", axis=0, tiled=True),
        lax.all_gather(upper, "row", axis=0, tiled=True),
    )
    dual_group, rhs_group = (
        lax.all_gather(dual_start, "col", axis=0, tiled=True),
        lax.all_gather(rhs, "col", axis=0, tiled=True),
    )
    primal_offset = lax.axis_index("row") * primal_len
    dual_offset = lax.axis_index("col") * dual_len
    for step in range(ITERS):
        pieces = dual_group.reshape(-1, side)[rows]
        prod = (
            jnp.einsum("kij,ki->kj", tiles, pieces, precision=lax.Precision.HIGHEST) * live[:, None]
        )
        grad = lax.psum(jax.ops.segment_sum(prod, cols, num_segments=col_blocks).reshape(-1), "row")
        primal_new = jnp.minimum(jnp.maximum(primal_group + tau * grad, lower_group), upper_group)
        extra = 2.0 * primal_new - primal_group
        apply_pieces = extra.reshape(-1, side)[cols]
        apply_prod = (
            jnp.einsum("kij,kj->ki", tiles, apply_pieces, precision=lax.Precision.HIGHEST)
            * live[:, None]
        )
        product = lax.psum(
            jax.ops.segment_sum(apply_prod, rows, num_segments=row_blocks).reshape(-1), "col"
        )
        resid = rhs_group - product
        dual_group = dual_group + sigma * resid
        moved_own = lax.dynamic_slice_in_dim(primal_new - primal_group, primal_offset, primal_len)
        resid_own = lax.dynamic_slice_in_dim(resid, dual_offset, dual_len)
        record(jnp.sum(resid_own * resid_own), jnp.sum(moved_own * moved_own))
        primal_group = primal_new
    primal_out = lax.dynamic_slice_in_dim(primal_group, primal_offset, primal_len)
    dual_out = lax.dynamic_slice_in_dim(dual_group, dual_offset, dual_len)
    norms = jnp.stack(records)
    return (primal_out, dual_out, norms)


def solution(mesh):
    in_specs = (
        P("col", "row", None, None, None),
        P("col", "row", None),
        P("col", "row", None),
        P("col", "row"),
        P(("row", "col")),
        P(("col", "row")),
        P(("col", "row")),
        P(("col", "row")),
        P(("row", "col")),
    )
    out_specs = (P(("col", "row")), P(("row", "col")), P())
    return jax.shard_map(local, mesh=mesh, in_specs=in_specs, out_specs=out_specs, check_vma=False)
```

profile of v0, /device:TPU:0, one launch (start us, length us, event | category | flops | bytes accessed | tf_op | source)
XLA Modules:
  0.0 321.8 jit_solution(8826910674664493860)
XLA Ops:
  0.6 0.0 copy-start
  0.6 0.0 copy-start.2
  0.7 0.0 copy-start.1
  0.7 0.8 reshape.230
  1.5 5.3 %all-gather = f32[2,1,1536]{2,1,0:T(1,128)S(1)} all-gather(f32[1,1,1536]{2,1,0:T(1,128)S(1)} %reshape.230), channel_id=1, replica_groups=mesh['col'=16,'row'=2] {'row'}, dimensions={0}, use_global_device_ids=true | all-gather | bytes 18432 | tf_op jit(solution)/shard_map/all_gather | solution.py:31
  6.8 0.7 reshape.236
  7.5 4.4 %all-gather.3 = f32[2,1,1536]{2,1,0:T(1,128)S(1)} all-gather(f32[1,1,1536]{2,1,0:T(1,128)S(1)} %reshape.236), channel_id=1, replica_groups=mesh['col'=16,'row'=2] {'row'}, dimensions={0}, use_global_device_ids=true | all-gather | bytes 18432 | tf_op jit(solution)/shard_map/all_gather | solution.py:33
  11.9 0.7 reshape.234
  12.6 4.4 %all-gather.2 = f32[2,1,1536]{2,1,0:T(1,128)S(1)} all-gather(f32[1,1,1536]{2,1,0:T(1,128)S(1)} %reshape.234), channel_id=1, replica_groups=mesh['col'=16,'row'=2] {'row'}, dimensions={0}, use_global_device_ids=true | all-gather | bytes 18432 | tf_op jit(solution)/shard_map/all_gather | solution.py:32
  16.9 22.4 %all-gather.1 = f32[16,1,512]{2,1,0:T(1,128)S(1)} all-gather(f32[1,1,512]{2,1,0:T(1,128)} %bitcast.129), channel_id=1, replica_groups=mesh['col'=16,'row'=2] {'col'}, dimensions={0}, use_global_device_ids=true | all-gather | bytes 34816 | tf_op jit(solution)/shard_map/all_gather | solution.py:36
  39.4 0.7 fusion.39
  40.1 0.6 gather_fusion
  40.6 0.0 copy-done
  40.6 1.4 fusion.10
  42.7 0.0 copy-done.2
  42.7 0.7 scatter_custom_fusion
  43.5 8.1 %psum.84 = f32[3072]{0:T(1024)S(1)} all-reduce(f32[3072]{0:T(1024)S(1)} %bitcast.126), channel_id=1, replica_groups=mesh['col'=16,'row'=2] {'row'}, use_global_device_ids=true, to_apply=%region_1.0 | all-reduce | flops 3072 | bytes 24576 | tf_op jit(solution)/shard_map/psum | solution.py:46
  51.6 0.0 copy-done.1
  51.6 17.2 %all-gather.4 = f32[16,1,512]{2,1,0:T(1,128)S(1)} all-gather(f32[1,1,512]{2,1,0:T(1,128)S(1)} %bitcast.130), channel_id=1, replica_groups=mesh['col'=16,'row'=2] {'col'}, dimensions={0}, use_global_device_ids=true | all-gather | bytes 34816 | tf_op jit(solution)/shard_map/all_gather | solution.py:37
  68.8 0.6 gather_fusion.1
  69.4 2.5 fusion.8
  71.9 0.9 scatter_custom_fusion.1
  72.8 59.4 %psum.85 = f32[8192]{0:T(1024)S(1)} all-reduce(f32[8192]{0:T(1024)S(1)} %bitcast.110), channel_id=1, replica_groups=mesh['col'=16,'row'=2] {'col'}, use_global_device_ids=true, to_apply=%region_3.0 | all-reduce | flops 8192 | bytes 65536 | tf_op jit(solution)/shard_map/psum | solution.py:54
  132.3 0.6 gather_fusion.2
  132.9 1.4 fusion.6
  134.3 0.7 scatter_custom_fusion.2
  135.0 7.1 %psum.86 = f32[3072]{0:T(1024)S(1)} all-reduce(f32[3072]{0:T(1024)S(1)} %bitcast.127), channel_id=1, replica_groups=mesh['col'=16,'row'=2] {'row'}, use_global_device_ids=true, to_apply=%region_5.0 | all-reduce | flops 3072 | bytes 24576 | tf_op jit(solution)/shard_map/psum | solution.py:46
  142.1 0.6 gather_fusion.3
  142.7 2.5 fusion.4
  145.2 0.9 scatter_custom_fusion.3
  146.1 57.6 %psum.87 = f32[8192]{0:T(1024)S(1)} all-reduce(f32[8192]{0:T(1024)S(1)} %bitcast.111), channel_id=1, replica_groups=mesh['col'=16,'row'=2] {'col'}, use_global_device_ids=true, to_apply=%region_7.0 | all-reduce | flops 8192 | bytes 65536 | tf_op jit(solution)/shard_map/psum | solution.py:54
  203.8 0.6 gather_fusion.4
  204.4 1.4 fusion.2
  205.8 0.7 scatter_custom_fusion.4
  206.5 8.1 %psum.88 = f32[3072]{0:T(1024)S(1)} all-reduce(f32[3072]{0:T(1024)S(1)} %bitcast.128), channel_id=1, replica_groups=mesh['col'=16,'row'=2] {'row'}, use_global_device_ids=true, to_apply=%region_9.0 | all-reduce | flops 3072 | bytes 24576 | tf_op jit(solution)/shard_map/psum | solution.py:46
  214.6 1.3 fusion.29
  216.0 0.6 gather_fusion.5
  216.6 2.5 fusion
  219.1 0.9 scatter_custom_fusion.5
  220.0 57.6 %psum.89 = f32[8192]{0:T(1024)S(1)} all-reduce(f32[8192]{0:T(1024)S(1)} %bitcast.109), channel_id=1, replica_groups=mesh['col'=16,'row'=2] {'col'}, use_global_device_ids=true, to_apply=%region_11.0 | all-reduce | flops 8192 | bytes 65536 | tf_op jit(solution)/shard_map/psum | solution.py:54
  277.6 1.3 multiply_reduce_fusion.2
  278.9 0.7 multiply_reduce_fusion.4
  279.6 37.3 %all-reduce = (f32[]{:T(128)}, f32[]{:T(128)}, f32[]{:T(128)}, f32[]{:T(128)}, f32[]{:T(128)}, /*index=5*/f32[]{:T(128)}) all-reduce(f32[]{:T(128)} %get-tuple-element.11, f32[]{:T(128)} %get-tuple-element.29, f32[]{:T(128)} %get-tuple-element.10, f32[]{:T(128)} %get-tuple-element.31, ...), channel_id=1, replica_groups=mesh['col'=16,'row'=2] {'col','row'}, use_global_device_ids=true, to_apply=%region_23.0 | all-reduce | flops 6 | bytes 48 | tf_op jit(solution)/shard_map/psum | solution.py:27
  318.2 0.1 maximum_bitcast_fusion.2
  319.6 0.1 maximum_bitcast_fusion.1
  321.0 0.1 maximum_bitcast_fusion
  321.1 0.7 copy.13
  (11 shorter events, 0.1 us)
Async XLA Ops:
  0.6 40.0 %copy-start = (f32[1,1,24,128,128]{4,3,2,1,0:T(8,128)S(1)}, f32[1,1,24,128,128]{4,3,2,1,0:T(8,128)}, u32[]{:S(2)}) copy-start(f32[1,1,24,128,128]{4,3,2,1,0:T(8,128)} %param.9) | copy-start | bytes 4718596
  0.6 42.1 %copy-start.2 = (s32[1,1,24]{2,1,0:T(1,128)S(1)}, s32[1,1,24]{2,1,0:T(1,128)}, u32[]{:S(2)}) copy-start(s32[1,1,24]{2,1,0:T(1,128)} %param.11) | copy-start | bytes 292
  0.7 50.9 %copy-start.1 = (f32[512]{0:T(512)S(1)}, f32[512]{0:T(512)}, u32[]{:S(2)}) copy-start(f32[512]{0:T(512)} %param.13) | copy-start | bytes 6148
where the time goes:
time: 323 us; the launch traced here: 322 us
  blocking collectives  289 us (89%)
  matrix products  11.9 us (4%)
  other arithmetic  9.14 us (3%)
  local copies, waits for them, and re-layouts  6.29 us (2%)
  between operations  5.46 us (2%)
    psum x3, blocking collectives, local(): lax.psum(jax.ops.segment_sum(apply_prod, rows, num_segments=row_blocks).r...  175 us
    psum x1, blocking collectives, record(): total_resid, total_moved = lax.psum((resid_sq, moved_sq), ('col', 'row'))  37.3 us
    psum x3, blocking collectives, local(): lax.psum(jax.ops.segment_sum(prod, cols, num_segments=col_blocks).reshape...  23.3 us
    all_gather x1, blocking collectives, local(): lax.all_gather(dual_start, 'col', axis=0, tiled=True)  22.4 us
    all_gather x1, blocking collectives, local(): lax.all_gather(rhs, 'col', axis=0, tiled=True)  17.2 us
    dot_general x3, matrix products, local(): jnp.einsum('kij,kj->ki', tiles, apply_pieces, precision=lax.Precision.HIG...  7.63 us

commit v1 on v0

v1 whole, which is shorter than its diff:
```python
import functools

import jax
import jax.numpy as jnp
from jax import lax
from jax.experimental import pallas as pl
from jax.experimental.pallas import tpu as pltpu
from jax.sharding import PartitionSpec as P

ITERS = 3
TAU = 0.4
SIGMA = 0.4
MESH = pl.DeviceIdType.MESH


def each(count, body):
    if count <= 32:
        for step in range(1, count):
            body(step)
    else:
        lax.fori_loop(1, count, lambda step, carry: (body(step), carry)[1], 0)


def split(value):
    high = value.astype(jnp.bfloat16).astype(jnp.float32)
    return high, value - high


def left_operand(value):
    high, low = split(value)
    first = jnp.concatenate([high, low], axis=0)
    second = jnp.concatenate([high, jnp.zeros_like(low)], axis=0)
    return jnp.concatenate([first, second], axis=1).astype(jnp.bfloat16)


def kernel(
    n_col, n_row,
    blocks, rows, cols, counts, rhs, lower, upper, primal, dual,
    primal_out, dual_out, norms_out,
    tiles, w_t, w_n, pieces,
    bounds, own_vec, y_buf, g_buf, p_send, p_recv, x_ref, z_ref, n_buf,
    load_sem, own_sem, bound_send, bound_recv, y_send_sem, y_recv_sem,
    g_send_sem, g_recv_sem, p_send_sem, p_recv_sem, n_send_sem, n_recv_sem,
):
    slots, side = tiles.shape[0], tiles.shape[1]
    dual_rows = dual.shape[0]
    primal_rows = primal.shape[0]
    row_blocks = dual_rows * n_col
    col_blocks = primal_rows * n_row
    total = n_col * n_row
    me_col = lax.axis_index("col")
    me_row = lax.axis_index("row")
    me = me_col * n_row + me_row

    load = pltpu.make_async_copy(blocks, tiles, load_sem)
    load.start()
    own_copies = []
    for index, source in enumerate((primal, lower, upper)):
        copy = pltpu.make_async_copy(source, bounds.at[index, me_row], own_sem.at[index])
        copy.start()
        own_copies.append(copy)
    for index, (source, target) in enumerate(((dual, y_buf.at[0, me_col]), (rhs, own_vec))):
        copy = pltpu.make_async_copy(source, target, own_sem.at[3 + index])
        copy.start()
        own_copies.append(copy)

    barrier = pltpu.get_barrier_semaphore()

    def greet(step):
        other = lax.rem(me + step, total)
        pl.semaphore_signal(
            barrier, inc=1, device_id=(other // n_row, lax.rem(other, n_row)), device_id_type=MESH
        )

    each(total, greet)
    pl.semaphore_wait(barrier, total - 1)

    def to_col(source, target, send, recv):
        def body(step):
            other = lax.rem(me_col + step, n_col)
            pltpu.make_async_remote_copy(
                src_ref=source(other), dst_ref=target, send_sem=send, recv_sem=recv,
                device_id=(other, me_row), device_id_type=MESH,
            ).start()

        each(n_col, body)

    def to_row(source, target, send, recv):
        def body(step):
            other = lax.rem(me_row + step, n_row)
            pltpu.make_async_remote_copy(
                src_ref=source, dst_ref=target, send_sem=send, recv_sem=recv,
                device_id=(me_col, other), device_id_type=MESH,
            ).start()

        each(n_row, body)

    def await_bytes(ref, sem):
        pltpu.make_async_copy(ref, ref, sem).wait()

    to_col(lambda other: dual, y_buf.at[0, me_col], y_send_sem.at[0], y_recv_sem.at[0])
    for index, source in enumerate((primal, lower, upper)):
        to_row(source, bounds.at[index, me_row], bound_send.at[index], bound_recv.at[index])

    load.wait()
    for k in range(slots):
        tile = tiles[k]
        high, low = split(tile)
        w_t[0:side, k * side : (k + 1) * side] = high.astype(jnp.bfloat16)
        w_t[side : 2 * side, k * side : (k + 1) * side] = low.astype(jnp.bfloat16)
        high, low = split(tile.T)
        w_n[0:side, k * side : (k + 1) * side] = high.astype(jnp.bfloat16)
        w_n[side : 2 * side, k * side : (k + 1) * side] = low.astype(jnp.bfloat16)

    live = counts[0, 0]
    row_of = [rows[0, k] for k in range(slots)]
    col_of = [cols[0, k] for k in range(slots)]
    row_to = [jnp.where(k < live, row_of[k], -1) for k in range(slots)]
    col_to = [jnp.where(k < live, col_of[k], -1) for k in range(slots)]

    def products(weights):
        left = left_operand(pieces[...])
        outs = []
        group = 4
        for base in range(0, slots, group):
            end = min(slots, base + group)
            result = jnp.dot(
                left, weights[:, base * side : end * side], preferred_element_type=jnp.float32
            )
            for k in range(base, end):
                at = slice((k - base) * side, (k - base + 1) * side)
                outs.append(result[k : k + 1, at] + result[slots + k : slots + k + 1, at])
        return outs

    def spread(outs, targets, count):
        places = lax.broadcasted_iota(jnp.int32, (count, side), 0)
        total_value = jnp.zeros((count, side), jnp.float32)
        for k in range(slots):
            total_value += jnp.where(places == targets[k], outs[k], 0.0)
        return total_value

    for copy in own_copies:
        copy.wait()
    for index in range(3):
        await_bytes(bounds.at[index, pl.ds(0, n_row - 1)], bound_recv.at[index])
    groups = []
    for index in range(3):
        groups.append(jnp.concatenate([bounds[index, r] for r in range(n_row)], axis=0))
    x_value, low_value, high_value = groups
    x_ref[0] = x_value
    x_ref[1] = low_value
    x_ref[2] = high_value
    y_own = y_buf[0, me_col]
    rhs_own = own_vec[...]
    owner = lax.broadcasted_iota(jnp.int32, (col_blocks, side), 0) // primal_rows
    sums = []

    for step in range(ITERS):
        await_bytes(y_buf.at[step, pl.ds(0, n_col - 1)], y_recv_sem.at[step])
        for k in range(slots):
            r = row_of[k]
            pieces[k : k + 1, :] = y_buf[step, r // dual_rows, pl.ds(lax.rem(r, dual_rows), 1), :]
        partial = spread(products(w_t), col_to, col_blocks)
        g_buf[step, me_row] = partial
        to_row(
            g_buf.at[step, me_row], g_buf.at[step, me_row], g_send_sem.at[step], g_recv_sem.at[step]
        )
        await_bytes(g_buf.at[step, pl.ds(0, n_row - 1)], g_recv_sem.at[step])
        grad = g_buf[step, 0]
        for r in range(1, n_row):
            grad += g_buf[step, r]
        x_old = x_ref[0]
        x_new = jnp.minimum(jnp.maximum(x_old + TAU * grad, x_ref[1]), x_ref[2])
        x_ref[0] = x_new
        z_ref[...] = 2.0 * x_new - x_old
        moved = jnp.where(owner == me_row, x_new - x_old, 0.0)
        for k in range(slots):
            pieces[k : k + 1, :] = z_ref[pl.ds(col_of[k], 1), :]
        applied = spread(products(w_n), row_to, row_blocks)
        for c in range(n_col):
            p_send[step, c] = applied[c * dual_rows : (c + 1) * dual_rows]
        to_col(
            lambda other: p_send.at[step, other], p_recv.at[step, me_col],
            p_send_sem.at[step], p_recv_sem.at[step],
        )
        p_recv[step, me_col] = p_send[step, me_col]
        moved_sum = jnp.sum(moved * moved, axis=0, keepdims=True)
        await_bytes(p_recv.at[step, pl.ds(0, n_col - 1)], p_recv_sem.at[step])
        product = p_recv[step, 0]
        for c in range(1, n_col):
            product += p_recv[step, c]
        resid = rhs_own - product
        y_own = y_own + SIGMA * resid
        if step + 1 < ITERS:
            y_buf[step + 1, me_col] = y_own
            to_col(
                lambda other: y_buf.at[step + 1, me_col], y_buf.at[step + 1, me_col],
                y_send_sem.at[step + 1], y_recv_sem.at[step + 1],
            )
        sums.append(jnp.sum(resid * resid, axis=0, keepdims=True))
        sums.append(moved_sum)

    table = jnp.sum(jnp.concatenate(sums, axis=0), axis=1, keepdims=True)
    table = jnp.broadcast_to(table, (2 * ITERS, side))
    at_row = lax.broadcasted_iota(jnp.int32, (2 * ITERS, side), 0)
    at_lane = lax.broadcasted_iota(jnp.int32, (2 * ITERS, side), 1)
    n_buf[me] = jnp.sum(jnp.where(at_row == at_lane, table, 0.0), axis=0, keepdims=True)

    def tell(step):
        other = lax.rem(me + step, total)
        pltpu.make_async_remote_copy(
            src_ref=n_buf.at[me], dst_ref=n_buf.at[me], send_sem=n_send_sem, recv_sem=n_recv_sem,
            device_id=(other // n_row, lax.rem(other, n_row)), device_id_type=MESH,
        ).start()

    each(total, tell)

    x_value = x_ref[0]
    mine = x_value[0:primal_rows]
    for r in range(1, n_row):
        mine = jnp.where(me_row == r, x_value[r * primal_rows : (r + 1) * primal_rows], mine)
    primal_out[...] = mine
    dual_out[...] = y_own

    await_bytes(y_buf.at[0, pl.ds(0, n_col - 1)], y_send_sem.at[0])
    for index in range(3):
        await_bytes(bounds.at[index, pl.ds(0, n_row - 1)], bound_send.at[index])
    for step in range(ITERS):
        if step:
            await_bytes(y_buf.at[step, pl.ds(0, n_col - 1)], y_send_sem.at[step])
        await_bytes(g_buf.at[step, pl.ds(0, n_row - 1)], g_send_sem.at[step])
        await_bytes(p_recv.at[step, pl.ds(0, n_col - 1)], p_send_sem.at[step])

    await_bytes(n_buf.at[pl.ds(0, total - 1)], n_recv_sem)
    norms = jnp.sqrt(jnp.sum(n_buf[...], axis=0))
    wide = jnp.broadcast_to(norms, (8, side))
    at_row = lax.broadcasted_iota(jnp.int32, (8, side), 0)
    at_lane = lax.broadcasted_iota(jnp.int32, (8, side), 1)
    first = jnp.sum(jnp.where(at_lane == 2 * at_row, wide, 0.0), axis=1, keepdims=True)
    second = jnp.sum(jnp.where(at_lane == 2 * at_row + 1, wide, 0.0), axis=1, keepdims=True)
    norms_out[...] = jnp.where(at_lane == 0, first, second)[0:ITERS, 0:2]
    await_bytes(n_buf.at[pl.ds(0, total - 1)], n_send_sem)


def local(blocks, row_index, col_index, counts, rhs, lower, upper, primal_start, dual_start):
    slots, side = blocks.shape[2], blocks.shape[3]
    n_col = lax.axis_size("col")
    n_row = lax.axis_size("row")
    primal_rows = primal_start.shape[0] // side
    dual_rows = dual_start.shape[0] // side
    row_blocks = dual_rows * n_col
    col_blocks = primal_rows * n_row
    hbm = pl.BlockSpec(memory_space=pltpu.HBM)
    smem = pl.BlockSpec(memory_space=pltpu.SMEM)
    vmem = pl.BlockSpec(memory_space=pltpu.VMEM)
    f32 = jnp.float32
    dma = pltpu.SemaphoreType.DMA
    primal, dual, norms = pl.pallas_call(
        functools.partial(kernel, n_col, n_row),
        out_shape=(
            jax.ShapeDtypeStruct((primal_rows, side), f32),
            jax.ShapeDtypeStruct((dual_rows, side), f32),
            jax.ShapeDtypeStruct((ITERS, 2), f32),
        ),
        in_specs=[hbm, smem, smem, smem, hbm, hbm, hbm, hbm, hbm],
        out_specs=(vmem, vmem, vmem),
        scratch_shapes=[
            pltpu.VMEM((slots, side, side), f32),
            pltpu.VMEM((2 * side, slots * side), jnp.bfloat16),
            pltpu.VMEM((2 * side, slots * side), jnp.bfloat16),
            pltpu.VMEM((slots, side), f32),
            pltpu.VMEM((3, n_row, primal_rows, side), f32),
            pltpu.VMEM((dual_rows, side), f32),
            pltpu.VMEM((ITERS, n_col, dual_rows, side), f32),
            pltpu.VMEM((ITERS, n_row, col_blocks, side), f32),
            pltpu.VMEM((ITERS, n_col, dual_rows, side), f32),
            pltpu.VMEM((ITERS, n_col, dual_rows, side), f32),
            pltpu.VMEM((3, col_blocks, side), f32),
            pltpu.VMEM((col_blocks, side), f32),
            pltpu.VMEM((n_col * n_row, 1, side), f32),
            dma, dma((5,)), dma((3,)), dma((3,)), dma((ITERS,)), dma((ITERS,)),
            dma((ITERS,)), dma((ITERS,)), dma((ITERS,)), dma((ITERS,)), dma, dma,
        ],
        compiler_params=pltpu.CompilerParams(collective_id=0, has_side_effects=True),
    )(
        blocks.reshape(slots, side, side),
        row_index.reshape(1, slots),
        col_index.reshape(1, slots),
        counts.reshape(1, 1),
        rhs.reshape(dual_rows, side),
        lower.reshape(primal_rows, side),
        upper.reshape(primal_rows, side),
        primal_start.reshape(primal_rows, side),
        dual_start.reshape(dual_rows, side),
    )
    return primal.reshape(-1), dual.reshape(-1), norms


def solution(mesh):
    in_specs = (
        P("col", "row", None, None, None),
        P("col", "row", None),
        P("col", "row", None),
        P("col", "row"),
        P(("row", "col")),
        P(("col", "row")),
        P(("col", "row")),
        P(("col", "row")),
        P(("row", "col")),
    )
    out_specs = (P(("col", "row")), P(("row", "col")), P())
    return jax.shard_map(local, mesh=mesh, in_specs=in_specs, out_specs=out_specs, check_vma=False)
```

time: 323 us -> 52.5 us (0.16)
  blocking collectives: 289 us -> 0 us
  Pallas kernels: 0 us -> 47.1 us
  matrix products: 11.9 us -> 0 us
  other arithmetic: 9.14 us -> 0 us
  between operations: 5.46 us -> 1.29 us
    psum x7 -> x0, blocking collectives: 235 us -> none  [the longest x3 175 us: local(): lax.psum(jax.ops.segment_sum(apply_prod, rows, num_segments=row_blocks).r...]
    all_gather x5 -> x0, blocking collectives: 53.7 us -> none  [the longest x1 22.4 us: local(): lax.all_gather(dual_start, 'col', axis=0, tiled=True)]
    pallas_call x0 -> x1, Pallas kernels: none -> 47.1 us  [local(): pl.pallas_call(functools.partial(kernel, n_col, n_row), out_shape=(jax.Sh...]
    dot_general x6 -> x0, matrix products: 11.9 us -> none  [the longest x3 7.63 us: local(): jnp.einsum('kij,kj->ki', tiles, apply_pieces, precision=lax.Precision.HIG...]
    scatter-add x6 -> x0, other arithmetic: 4.88 us -> none  [the longest x3 2.68 us: local(): jax.ops.segment_sum(apply_prod, rows, num_segments=row_blocks).reshape(-1)]
    gather x6 -> x0, local copies, waits for them, and re-layouts: 3.4 us -> none  [the longest x3 1.7 us: local(): pieces = dual_group.reshape(-1, side)[rows]]
    reduce_sum x3 -> x0, other arithmetic: 3.28 us -> none  [local(): record(jnp.sum(resid_own * resid_own), jnp.sum(moved_own * moved_own))]
where the time goes in v1:
time: 52.5 us; the launch traced here: 52.2 us
  Pallas kernels  47.1 us (90%)
  local copies, waits for them, and re-layouts  3.83 us (7%)
  between operations  1.29 us (2%)
    pallas_call x1, Pallas kernels, local(): pl.pallas_call(functools.partial(kernel, n_col, n_row), out_shape=(jax.Sh...  47.1 us
    unnamed x3, local copies, waits for them, and re-layouts  3.83 us

profile of v1, /device:TPU:0, one launch (start us, length us, event | category | flops | bytes accessed | tf_op | source)
XLA Modules:
  0.0 52.2 jit_solution(1279009220801227719)
XLA Ops:
  1.3 47.1 %shard_map.112 = (f32[12,128]{1,0:T(8,128)}, f32[4,128]{1,0:T(4,128)}, f32[3,2]{1,0:T(4,128)}) custom-call(f32[24,128,128]{2,1,0:T(8,128)} %bitcast.10, s32[1,24]{1,0:T(1,128)} %bitcast.18, s32[1,24]{1,0:T(1,128)} %bitcast.19, s32[1,1]{1,0:T(1,128)S(6)} %copy.15.counts, f32[4,128]{1,0:T(4,128)} %bitcast.15, f32[12,128]{1,0:T(8,128)} %bitcast.11, ...), custom_call_target="tpu_custom_call" | custom-call | tf_op jit(solution)/shard_map/pallas_call | solution.py:258
  48.4 1.3 %copy.12 = f32[3,2]{0,1:T(2,128)} copy(f32[3,2]{1,0:T(4,128)} %get-tuple-element.11) | data formatting | bytes 48
  49.7 1.3 %copy.16 = f32[1536]{0:T(1024)} copy(f32[1536]{0:T(1024)} %bitcast.14) | data formatting | bytes 12288
  51.0 1.2 %copy.17 = f32[512]{0:T(512)} copy(f32[512]{0:T(512)} %bitcast.17) | data formatting | bytes 4096

commit v2 on v1

--- a/solution.py
+++ b/solution.py
@@ -66,14 +66,17 @@
 
     barrier = pltpu.get_barrier_semaphore()
 
-    def greet(step):
-        other = lax.rem(me + step, total)
-        pl.semaphore_signal(
-            barrier, inc=1, device_id=(other // n_row, lax.rem(other, n_row)), device_id_type=MESH
-        )
-
-    each(total, greet)
-    pl.semaphore_wait(barrier, total - 1)
+    def greet_col(step):
+        other = (lax.rem(me_col + step, n_col), me_row)
+        pl.semaphore_signal(barrier, inc=1, device_id=other, device_id_type=MESH)
+
+    def greet_row(step):
+        other = (me_col, lax.rem(me_row + step, n_row))
+        pl.semaphore_signal(barrier, inc=1, device_id=other, device_id_type=MESH)
+
+    each(n_col, greet_col)
+    each(n_row, greet_row)
+    pl.semaphore_wait(barrier, n_col + n_row - 2)
 
     def to_col(source, target, send, recv):
         def body(step):
@@ -98,9 +101,11 @@
     def await_bytes(ref, sem):
         pltpu.make_async_copy(ref, ref, sem).wait()
 
-    to_col(lambda other: dual, y_buf.at[0, me_col], y_send_sem.at[0], y_recv_sem.at[0])
+    own_copies[3].wait()
+    to_col(lambda other: y_buf.at[0, me_col], y_buf.at[0, me_col], y_send_sem.at[0], y_recv_sem.at[0])
     for index, source in enumerate((primal, lower, upper)):
-        to_row(source, bounds.at[index, me_row], bound_send.at[index], bound_recv.at[index])
+        own_copies[index].wait()
+        to_row(bounds.at[index, me_row], bounds.at[index, me_row], bound_send.at[index], bound_recv.at[index])
 
     load.wait()
     for k in range(slots):
@@ -119,17 +124,18 @@
     col_to = [jnp.where(k < live, col_of[k], -1) for k in range(slots)]
 
     def products(weights):
-        left = left_operand(pieces[...])
         outs = []
-        group = 4
+        group = 8
         for base in range(0, slots, group):
             end = min(slots, base + group)
+            left = left_operand(pieces[base:end, :])
             result = jnp.dot(
                 left, weights[:, base * side : end * side], preferred_element_type=jnp.float32
             )
-            for k in range(base, end):
-                at = slice((k - base) * side, (k - base + 1) * side)
-                outs.append(result[k : k + 1, at] + result[slots + k : slots + k + 1, at])
+            for k in range(end - base):
+                at = slice(k * side, (k + 1) * side)
+                low = end - base + k
+                outs.append(result[k : k + 1, at] + result[low : low + 1, at])
         return outs
 
     def spread(outs, targets, count):
@@ -139,8 +145,7 @@
             total_value += jnp.where(places == targets[k], outs[k], 0.0)
         return total_value
 
-    for copy in own_copies:
-        copy.wait()
+    own_copies[4].wait()
     for index in range(3):
         await_bytes(bounds.at[index, pl.ds(0, n_row - 1)], bound_recv.at[index])
     groups = []
@@ -236,10 +241,33 @@
     wide = jnp.broadcast_to(norms, (8, side))
     at_row = lax.broadcasted_iota(jnp.int32, (8, side), 0)
     at_lane = lax.broadcasted_iota(jnp.int32, (8, side), 1)
-    first = jnp.sum(jnp.where(at_lane == 2 * at_row, wide, 0.0), axis=1, keepdims=True)
-    second = jnp.sum(jnp.where(at_lane == 2 * at_row + 1, wide, 0.0), axis=1, keepdims=True)
-    norms_out[...] = jnp.where(at_lane == 0, first, second)[0:ITERS, 0:2]
+    outputs = jnp.zeros((8, side), jnp.float32)
+    for k in range(ITERS):
+        chosen = jnp.where(at_lane == 2 * k + at_row, wide, 0.0)
+        outputs = jnp.where(at_lane == k, jnp.sum(chosen, axis=1, keepdims=True), outputs)
+    norms_out[...] = outputs
     await_bytes(n_buf.at[pl.ds(0, total - 1)], n_send_sem)
+
+
+def finish_kernel(primal, dual, norms, primal_out, dual_out, norms_out):
+    primal_out[...] = primal[...]
+    dual_out[...] = dual[...]
+    norms_out[...] = norms[0:2, 0:ITERS]
+
+
+def finish(primal, dual, norms):
+    vmem = pl.BlockSpec(memory_space=pltpu.VMEM)
+    primal, dual, norms = pl.pallas_call(
+        finish_kernel,
+        out_shape=(
+            jax.ShapeDtypeStruct(primal.shape, jnp.float32),
+            jax.ShapeDtypeStruct(dual.shape, jnp.float32),
+            jax.ShapeDtypeStruct((2, ITERS), jnp.float32),
+        ),
+        in_specs=[vmem] * 3,
+        out_specs=(vmem,) * 3,
+    )(primal, dual, norms)
+    return primal.reshape(-1), dual.reshape(-1), norms.T
 
 
 def local(blocks, row_index, col_index, counts, rhs, lower, upper, primal_start, dual_start):
@@ -260,7 +288,7 @@
         out_shape=(
             jax.ShapeDtypeStruct((primal_rows, side), f32),
             jax.ShapeDtypeStruct((dual_rows, side), f32),
-            jax.ShapeDtypeStruct((ITERS, 2), f32),
+            jax.ShapeDtypeStruct((8, side), f32),
         ),
         in_specs=[hbm, smem, smem, smem, hbm, hbm, hbm, hbm, hbm],
         out_specs=(vmem, vmem, vmem),
@@ -293,7 +321,7 @@
         primal_start.reshape(primal_rows, side),
         dual_start.reshape(dual_rows, side),
     )
-    return primal.reshape(-1), dual.reshape(-1), norms
+    return finish(primal, dual, norms)
 
 
 def solution(mesh):

time: 52.5 us -> 48.7 us (0.928)
  local copies, waits for them, and re-layouts: 3.83 us -> 0 us
    unnamed x3 -> x0, local copies, waits for them, and re-layouts: 3.83 us -> none
    pallas_call x0 -> x1, Pallas kernels: none -> 1.31 us  [finish(): pl.pallas_call(finish_kernel, out_shape=(jax.ShapeDtypeStruct(primal.shap...]
    pallas_call x1, Pallas kernels: 47.1 us -> 45.9 us  [local(): pl.pallas_call(functools.partial(kernel, n_col, n_row), out_shape=(jax.Sh...]
where the time goes in v2:
time: 48.7 us; the launch traced here: 48.5 us
  Pallas kernels  47.2 us (97%)
  between operations  1.29 us (3%)
    pallas_call x1, Pallas kernels, local(): pl.pallas_call(functools.partial(kernel, n_col, n_row), out_shape=(jax.Sh...  45.9 us
    pallas_call x1, Pallas kernels, finish(): pl.pallas_call(finish_kernel, out_shape=(jax.ShapeDtypeStruct(primal.shap...  1.31 us

profile of v2, /device:TPU:0, one launch (start us, length us, event | category | flops | bytes accessed | tf_op | source)
XLA Modules:
  0.0 48.5 jit_solution(9396457380596216183)
XLA Ops:
  1.3 45.9 %shard_map.112 = (f32[12,128]{1,0:T(8,128)}, f32[4,128]{1,0:T(4,128)}, f32[8,128]{1,0:T(8,128)}) custom-call(f32[24,128,128]{2,1,0:T(8,128)} %bitcast.11, s32[1,24]{1,0:T(1,128)} %bitcast.17, s32[1,24]{1,0:T(1,128)} %bitcast.18, s32[1,1]{1,0:T(1,128)S(6)} %copy.12.counts, f32[4,128]{1,0:T(4,128)} %bitcast.15, f32[12,128]{1,0:T(8,128)} %bitcast.12, ...), custom_call_target="tpu_custom_call" | custom-call | tf_op jit(solution)/shard_map/pallas_call | solution.py:286
  47.2 1.3 %shard_map.113 = (f32[12,128]{1,0:T(8,128)}, f32[4,128]{1,0:T(4,128)}, f32[2,3]{1,0:T(2,128)}) custom-call(f32[12,128]{1,0:T(8,128)} %get-tuple-element.9.primal, f32[4,128]{1,0:T(4,128)} %get-tuple-element.10.dual, f32[8,128]{1,0:T(8,128)} %get-tuple-element.11.norms), custom_call_target="tpu_custom_call" | custom-call | tf_op jit(solution)/shard_map/pallas_call | solution.py:260
